TPU v7x, 32 devices: a whole 2x2x4 slice. The times are simulated.
32 devices in a mesh: gx: 16 (over z, y, core), gy: 2 (over x).
Axes of the slice: x: 2, y: 2, z: 4, core: 2. Of those that a mesh axis runs over, the one named last changes fastest.
Arguments:
- populations: float32 [19, 64, 16, 128], P(None, 'gx', 'gy'), may hold values from 0.02 to 0.1
- fluid: int32 [64, 16, 128], P('gx', 'gy'), may hold values 0 or 1
Outputs:
- advanced: float32 [19, 64, 16, 128], P(None, 'gx', 'gy')
Inputs may be any that keep to these rules, and one draw needn't show every extreme that they name: 1 marks a fluid cell, 0 a solid one.
All inputs are finite; a program needn't handle non-finite values. No bound on the sum of `fluid` on one device may be relied on, other than what follows from the above.
Results may differ from a plain program's by a relative error of at most 0.0001.
Values sent between devices are 32-bit elements; how exact they have to be, the bound alone decides.
A program may use at most 64 MiB of HBM per device.

v0:
```python
import functools

import jax
import jax.numpy as jnp
import numpy as np
from jax import lax
from jax.experimental import pallas as pl
from jax.experimental.pallas import tpu as pltpu
from jax.sharding import PartitionSpec as P

STEPS = 4
DEPTH = 4
PAD = 8
RELAX = 1.25

VEL = [
    (0, 0, 0), (0, 0, 1), (0, 0, -1),
    (0, -1, 0), (0, -1, 1), (0, -1, -1),
    (0, 1, 0), (0, 1, 1), (0, 1, -1),
    (1, 1, 0), (1, 0, 0), (1, 0, 1), (1, 0, -1), (1, -1, 0),
    (-1, -1, 0), (-1, 0, 0), (-1, 0, 1), (-1, 0, -1), (-1, 1, 0),
]
REFERENCE_VEL = [
    (0, 0, 0), (1, 0, 0), (-1, 0, 0), (0, 1, 0), (0, -1, 0), (0, 0, 1), (0, 0, -1),
    (1, 1, 0), (-1, -1, 0), (1, -1, 0), (-1, 1, 0), (1, 0, 1), (-1, 0, -1),
    (1, 0, -1), (-1, 0, 1), (0, 1, 1), (0, -1, -1), (0, 1, -1), (0, -1, 1),
]
TO_REF = [REFERENCE_VEL.index(v) for v in VEL]
OPP = [VEL.index((-x, -y, -z)) for x, y, z in VEL]
WEIGHT = [(1.0 / 3.0, 1.0 / 18.0, 1.0 / 36.0)[abs(x) + abs(y) + abs(z)] for x, y, z in VEL]
DIRECTIONS = [(1, 0), (-1, 0), (0, 1), (0, -1), (1, 1), (1, -1), (-1, 1), (-1, -1)]


def runs(dx, dy):
    picks = [q for q in range(19) if (not dx or VEL[q][0] == dx) and (not dy or VEL[q][1] == dy)]
    result = []
    for q in picks:
        if result and result[-1][1] == q:
            result[-1][1] = q + 1
        else:
            result.append([q, q + 1])
    return result


def spans(d, offset, length, depth):
    if d == 0:
        return [(offset, offset, length, False)]
    inner = depth - 1
    if d > 0:
        full = (offset + length - inner, offset - inner, inner, False)
        edge = (offset + length - depth, offset - depth, 1, True)
    else:
        full = (offset, offset + length, inner, False)
        edge = (offset + inner, offset + length + inner, 1, True)
    return [full, edge] if inner else [edge]


def pieces(dx, dy, sizes, depth):
    lx, ly = sizes
    result = []
    for xs, xt, xn, xedge in spans(dx, depth, lx, depth):
        for ys, yt, yn, yedge in spans(dy, PAD, ly, depth):
            for lo, hi in runs(dx if xedge else 0, dy if yedge else 0):
                result.append((lo, hi - lo, xs, xt, xn, ys, yt, yn))
    return result


def mark_piece(dx, dy, sizes, depth):
    def along(d, offset, length):
        if d == 0:
            return offset, offset, length
        if d > 0:
            return offset + length - depth, offset - depth, depth
        return offset, offset + length, depth

    return along(dx, depth, sizes[0]) + along(dy, PAD, sizes[1])


def collide(f):
    pairs = [(q, OPP[q]) for q in range(1, 19) if q < OPP[q]]
    rho = f[0]
    moment = [None, None, None]
    for i, j in pairs:
        rho = rho + (f[i] + f[j])
        diff = f[i] - f[j]
        for axis in range(3):
            c = VEL[i][axis]
            if c:
                term = moment[axis]
                if term is None:
                    moment[axis] = diff if c > 0 else -diff
                else:
                    moment[axis] = term + diff if c > 0 else term - diff
    inverse = 1.0 / rho
    u = [m * inverse for m in moment]
    base = 1.0 - 1.5 * (u[0] * u[0] + u[1] * u[1] + u[2] * u[2])
    scaled = {w: (RELAX * w) * rho for w in set(WEIGHT)}
    keep = 1.0 - RELAX
    post = [None] * 19
    post[0] = keep * f[0] + scaled[WEIGHT[0]] * base
    for i, j in pairs:
        proj = None
        for axis in range(3):
            c = VEL[i][axis]
            if c:
                if proj is None:
                    proj = u[axis] if c > 0 else -u[axis]
                else:
                    proj = proj + u[axis] if c > 0 else proj - u[axis]
        even = scaled[WEIGHT[i]] * (base + 4.5 * (proj * proj))
        odd = scaled[WEIGHT[i]] * (3.0 * proj)
        post[i] = keep * f[i] + (even + odd)
        post[j] = keep * f[j] + (even - odd)
    return post


def row_starts(ring, ly):
    first, last = PAD - ring, PAD + ly + ring
    starts = list(range(first, last - 7, 8))
    if starts[-1] + 8 < last:
        starts.append(last - 8)
    return starts


def stream(buf, marks, layer, row):
    result = []
    for q, (cx, cy, cz) in enumerate(VEL):
        if q == 0:
            result.append(buf[0, layer, pl.ds(row, 8), :])
            continue
        source = buf[q, layer - cx, pl.ds(row - cy, 8), :]
        if cz:
            source = pltpu.roll(source, cz % source.shape[-1], 1)
        open_ = marks[cz % 3, layer - cx, pl.ds(row - cy, 8), :] != 0
        result.append(jnp.where(open_, source, buf[OPP[q], layer, pl.ds(row, 8), :]))
    return result


def kernel(axes, sizes, depth, pops_hbm, fluid_hbm, out_hbm, first, last_f, marks, *rest):
    rounds = STEPS // depth
    bufs, rest = rest[:rounds], rest[rounds:]
    inner, rest = rest[: depth - 1], rest[depth - 1 :]
    in_sem, out_sem, mark_send, mark_recv, send_sem, recv_sem = rest
    lx, ly = sizes
    nx, ny = axes
    ix, iy = lax.axis_index("gx"), lax.axis_index("gy")
    has = {0: None, 1: iy < ny - 1, -1: iy > 0}

    def when(condition, action):
        if condition is None:
            action()
        else:
            pl.when(condition)(action)

    def target(dx, dy):
        return {"gx": lax.rem(ix + nx + dx, nx), "gy": iy + dy}

    fluid_in = pltpu.make_async_copy(
        fluid_hbm, marks.at[0, pl.ds(depth, lx), pl.ds(PAD, ly)], in_sem.at[lx]
    )
    loads = [
        pltpu.make_async_copy(pops_hbm.at[:, a], first.at[:, a], in_sem.at[a]) for a in range(lx)
    ]

    barrier = pltpu.get_barrier_semaphore()
    for dx, dy in DIRECTIONS:
        when(
            has[dy],
            lambda dx=dx, dy=dy: pl.semaphore_signal(
                barrier, inc=1, device_id=target(dx, dy), device_id_type=pl.DeviceIdType.MESH
            ),
        )

    fluid_in.start()
    for load in loads:
        load.start()

    for edge, rows in ((iy == 0, PAD - depth), (iy == ny - 1, PAD + ly)):

        @pl.when(edge)
        def _():
            for a in range(lx + 2 * depth):
                marks[0, a, rows : rows + depth, :] = jnp.zeros((depth, marks.shape[-1]), jnp.int32)

    def post_layer(a):
        f = [first[TO_REF[q], a] for q in range(19)]
        for q, value in enumerate(collide(f)):
            bufs[0][q, depth + a, PAD : PAD + ly, :] = value

    order = sorted(range(lx), key=lambda a: min(a, lx - 1 - a))
    for a in order:
        loads[a].wait()
        post_layer(a)
    fluid_in.wait()

    peers = 2 + 3 * (iy > 0).astype(jnp.int32) + 3 * (iy < ny - 1).astype(jnp.int32)
    pl.semaphore_wait(barrier, peers)

    def exchange(copies):
        for (dx, dy), group in copies:
            when(has[dy], lambda group=group: [c.start() for c in group] and None)

    def arrive(copies):
        for (dx, dy), group in copies:
            when(has[-dy], lambda group=group: [c.wait_recv() for c in group] and None)

    def drain(copies):
        for (dx, dy), group in copies:
            when(has[dy], lambda group=group: [c.wait_send() for c in group] and None)

    def mark_copies():
        result = []
        for i, (dx, dy) in enumerate(DIRECTIONS):
            xs, xt, xn, ys, yt, yn = mark_piece(dx, dy, sizes, depth)
            result.append(
                (
                    (dx, dy),
                    [
                        pltpu.make_async_remote_copy(
                            src_ref=marks.at[0, pl.ds(xs, xn), pl.ds(ys, yn)],
                            dst_ref=marks.at[0, pl.ds(xt, xn), pl.ds(yt, yn)],
                            send_sem=mark_send.at[i],
                            recv_sem=mark_recv.at[i],
                            device_id=target(dx, dy),
                            device_id_type=pl.DeviceIdType.MESH,
                        )
                    ],
                )
            )
        return result

    def halo_copies(turn):
        buf = bufs[turn]
        result, count = [], 0
        for dx, dy in DIRECTIONS:
            group = []
            for lo, n, xs, xt, xn, ys, yt, yn in pieces(dx, dy, sizes, depth):
                group.append(
                    pltpu.make_async_remote_copy(
                        src_ref=buf.at[pl.ds(lo, n), pl.ds(xs, xn), pl.ds(ys, yn)],
                        dst_ref=buf.at[pl.ds(lo, n), pl.ds(xt, xn), pl.ds(yt, yn)],
                        send_sem=send_sem.at[turn, count],
                        recv_sem=recv_sem.at[turn, count],
                        device_id=target(dx, dy),
                        device_id_type=pl.DeviceIdType.MESH,
                    )
                )
                count += 1
            result.append(((dx, dy), group))
        return result

    mark_list = mark_copies()
    exchange(mark_list)
    halos = [halo_copies(turn) for turn in range(rounds)]
    exchange(halos[0])

    arrive(mark_list)
    for a in range(lx + 2 * depth):
        for row in row_starts(depth, ly):
            here = marks[0, a, row : row + 8, :]
            lanes = here.shape[-1]
            marks[1, a, row : row + 8, :] = pltpu.roll(here, 1, 1)
            marks[2, a, row : row + 8, :] = pltpu.roll(here, lanes - 1, 1)

    stores = []
    for turn in range(rounds):
        arrive(halos[turn])
        source = bufs[turn]
        for ring in range(depth - 1, -1, -1):
            final = turn == rounds - 1 and ring == 0
            for a in range(-ring, lx + ring):
                for row in row_starts(ring, ly):
                    f = stream(source, marks, depth + a, row)
                    if final:
                        wet = marks[0, depth + a, row : row + 8, :] != 0
                        for q in range(19):
                            old = first[TO_REF[q], a, row - PAD : row - PAD + 8, :]
                            last_f[TO_REF[q], a, row - PAD : row - PAD + 8, :] = jnp.where(
                                wet, f[q], old
                            )
                    else:
                        into = inner[ring - 1] if ring else bufs[turn + 1]
                        for q, value in enumerate(collide(f)):
                            into[q, depth + a, row : row + 8, :] = value
                if final:
                    store = pltpu.make_async_copy(last_f.at[:, a], out_hbm.at[:, a], out_sem.at[a])
                    store.start()
                    stores.append(store)
            if ring:
                source = inner[ring - 1]
        if turn + 1 < rounds:
            exchange(halos[turn + 1])
    drain(mark_list)
    for turn in range(rounds):
        drain(halos[turn])
    for store in stores:
        store.wait()


def per_device(axes, depth, populations, fluid):
    sizes = fluid.shape[:2]
    lx, ly = sizes
    nz = fluid.shape[2]
    rounds = STEPS // depth
    wide = (lx + 2 * depth, ly + 2 * PAD, nz)
    count = sum(len(pieces(dx, dy, sizes, depth)) for dx, dy in DIRECTIONS)
    dma = pltpu.SemaphoreType.DMA
    return pl.pallas_call(
        functools.partial(kernel, axes, sizes, depth),
        out_shape=jax.ShapeDtypeStruct(populations.shape, populations.dtype),
        in_specs=[pl.BlockSpec(memory_space=pl.ANY)] * 2,
        out_specs=pl.BlockSpec(memory_space=pl.ANY),
        scratch_shapes=[
            pltpu.VMEM(populations.shape, jnp.float32),
            pltpu.VMEM(populations.shape, jnp.float32),
            pltpu.VMEM((3,) + wide, jnp.int32),
        ]
        + [pltpu.VMEM((19,) + wide, jnp.float32)] * (rounds + depth - 1)
        + [
            dma((lx + 1,)),
            dma((lx,)),
            dma((len(DIRECTIONS),)),
            dma((len(DIRECTIONS),)),
            dma((rounds, count)),
            dma((rounds, count)),
        ],
        compiler_params=pltpu.CompilerParams(collective_id=0, has_side_effects=True),
    )(populations, fluid)


def solution(mesh):
    axes = (mesh.shape["gx"], mesh.shape["gy"])
    return jax.shard_map(
        functools.partial(per_device, axes, DEPTH),
        mesh=mesh,
        in_specs=(P(None, "gx", "gy", None), P("gx", "gy", None)),
        out_specs=P(None, "gx", "gy", None),
        check_vma=False,
    )
```

profile of v0, /device:TPU:1, one launch (start us, length us, event | category | flops | bytes accessed | tf_op | source)
XLA Modules:
  0.0 18.3 jit_solution(3463298206039673183)
XLA Ops:
  0.0 16.6 %shard_map.28 = f32[19,4,8,128]{3,2,1,0:T(8,128)} custom-call(f32[19,4,8,128]{3,2,1,0:T(8,128)} %pops_hbm.1, s32[4,8,128]{2,1,0:T(8,128)} %fluid_hbm.1), custom_call_target="tpu_custom_call" | custom-call | tf_op jit(solution)/shard_map/pallas_call | solution.py:308
  16.6 1.7 %copy.4 = f32[19,4,8,128]{3,2,1,0:T(8,128)} copy(f32[19,4,8,128]{3,2,1,0:T(8,128)} %shard_map.28) | data formatting | bytes 622592
where the time goes:
time: 18.5 us; the launch traced here: 18.3 us
  Pallas kernels  16.6 us (90%)
  local copies, waits for them, and re-layouts  1.71 us (9%)
    pallas_call x1, Pallas kernels, per_device(): pl.pallas_call(functools.partial(kernel, axes, sizes, depth), out_shape=j...  16.6 us
    unnamed x1, local copies, waits for them, and re-layouts  1.71 us

commit v1 on v0

--- a/solution.py
+++ b/solution.py
@@ -275,7 +275,7 @@
                         wet = marks[0, depth + a, row : row + 8, :] != 0
                         for q in range(19):
                             old = first[TO_REF[q], a, row - PAD : row - PAD + 8, :]
-                            last_f[TO_REF[q], a, row - PAD : row - PAD + 8, :] = jnp.where(
+                            out_hbm[TO_REF[q], a, row - PAD : row - PAD + 8, :] = jnp.where(
                                 wet, f[q], old
                             )
                     else:
@@ -283,9 +283,7 @@
                         for q, value in enumerate(collide(f)):
                             into[q, depth + a, row : row + 8, :] = value
                 if final:
-                    store = pltpu.make_async_copy(last_f.at[:, a], out_hbm.at[:, a], out_sem.at[a])
-                    store.start()
-                    stores.append(store)
+                    store = None
             if ring:
                 source = inner[ring - 1]
         if turn + 1 < rounds:
@@ -305,11 +303,11 @@
     wide = (lx + 2 * depth, ly + 2 * PAD, nz)
     count = sum(len(pieces(dx, dy, sizes, depth)) for dx, dy in DIRECTIONS)
     dma = pltpu.SemaphoreType.DMA
-    return pl.pallas_call(
+    mid = pl.pallas_call(
         functools.partial(kernel, axes, sizes, depth),
-        out_shape=jax.ShapeDtypeStruct(populations.shape, populations.dtype),
+        out_shape=pltpu.VMEM(populations.shape, populations.dtype),
         in_specs=[pl.BlockSpec(memory_space=pl.ANY)] * 2,
-        out_specs=pl.BlockSpec(memory_space=pl.ANY),
+        out_specs=pl.BlockSpec(memory_space=pltpu.VMEM),
         scratch_shapes=[
             pltpu.VMEM(populations.shape, jnp.float32),
             pltpu.VMEM(populations.shape, jnp.float32),
@@ -324,8 +322,15 @@
             dma((rounds, count)),
             dma((rounds, count)),
         ],
-        compiler_params=pltpu.CompilerParams(collective_id=0, has_side_effects=True),
+        compiler_params=pltpu.CompilerParams(collective_id=0, has_side_effects=True, vmem_limit_bytes=60 * 1024 * 1024),
     )(populations, fluid)
+    def k2(x, o, sem):
+        cs=[pltpu.make_async_copy(x.at[:, a], o.at[:, a], sem.at[a]) for a in range(lx)]
+        for c in cs: c.start()
+        for c in cs: c.wait()
+    return pl.pallas_call(k2, out_shape=jax.ShapeDtypeStruct(populations.shape, populations.dtype),
+        in_specs=[pl.BlockSpec(memory_space=pltpu.VMEM)], out_specs=pl.BlockSpec(memory_space=pl.ANY),
+        scratch_shapes=[dma((lx,))], compiler_params=pltpu.CompilerParams(vmem_limit_bytes=16*2**20))(mid)
 
 
 def solution(mesh):

time: 18.5 us -> 16.9 us (0.914)
  local copies, waits for them, and re-layouts: 1.71 us -> 0 us
    unnamed x1 -> x0, local copies, waits for them, and re-layouts: 1.71 us -> none
    pallas_call x1 -> x2, Pallas kernels: 16.6 us -> 16.7 us  [the longest x1 16 us: per_device(): pl.pallas_call(functools.partial(kernel, axes, sizes, depth), out_shape=p...]
where the time goes in v1:
time: 16.9 us; the launch traced here: 16.7 us
  Pallas kernels  16.7 us (99%)
    pallas_call x1, Pallas kernels, per_device(): pl.pallas_call(functools.partial(kernel, axes, sizes, depth), out_shape=p...  16 us
    pallas_call x1, Pallas kernels, per_device(): pl.pallas_call(k2, out_shape=jax.ShapeDtypeStruct(populations.shape, popu...  0.75 us

profile of v1, /device:TPU:1, one launch (start us, length us, event | category | flops | bytes accessed | tf_op | source)
XLA Modules:
  0.0 16.7 jit_solution(5184359128532630604)
XLA Ops:
  0.0 16.0 %shard_map.28.x = f32[19,4,8,128]{3,2,1,0:T(8,128)S(1)} custom-call(f32[19,4,8,128]{3,2,1,0:T(8,128)} %pops_hbm.1, s32[4,8,128]{2,1,0:T(8,128)} %fluid_hbm.1), custom_call_target="tpu_custom_call" | custom-call | tf_op jit(solution)/shard_map/pallas_call | solution.py:306
  16.0 0.7 %shard_map.29 = f32[19,4,8,128]{3,2,1,0:T(8,128)} custom-call(f32[19,4,8,128]{3,2,1,0:T(8,128)S(1)} %shard_map.28.x), custom_call_target="tpu_custom_call" | custom-call | tf_op jit(solution)/shard_map/pallas_call | solution.py:331

commit v2 on v0

v2 whole, which is shorter than its diff:
```python
import functools

import jax
import jax.numpy as jnp
import numpy as np
from jax import lax
from jax.experimental import pallas as pl
from jax.experimental.pallas import tpu as pltpu
from jax.sharding import PartitionSpec as P

STEPS = 4
HALO = 4
PAD = 8
RELAX = 1.25

VEL = [
    (0, 0, 0), (0, 0, 1), (0, 0, -1),
    (0, -1, 0), (0, -1, 1), (0, -1, -1),
    (0, 1, 0), (0, 1, 1), (0, 1, -1),
    (1, 1, 0), (1, 0, 0), (1, 0, 1), (1, 0, -1), (1, -1, 0),
    (-1, -1, 0), (-1, 0, 0), (-1, 0, 1), (-1, 0, -1), (-1, 1, 0),
]
REFERENCE_VEL = [
    (0, 0, 0), (1, 0, 0), (-1, 0, 0), (0, 1, 0), (0, -1, 0), (0, 0, 1), (0, 0, -1),
    (1, 1, 0), (-1, -1, 0), (1, -1, 0), (-1, 1, 0), (1, 0, 1), (-1, 0, -1),
    (1, 0, -1), (-1, 0, 1), (0, 1, 1), (0, -1, -1), (0, 1, -1), (0, -1, 1),
]
TO_REF = [REFERENCE_VEL.index(v) for v in VEL]
OPP = [VEL.index((-x, -y, -z)) for x, y, z in VEL]
WEIGHT = [(1.0 / 3.0, 1.0 / 18.0, 1.0 / 36.0)[abs(x) + abs(y) + abs(z)] for x, y, z in VEL]
DIRECTIONS = [(1, 0), (-1, 0), (0, 1), (0, -1), (1, 1), (1, -1), (-1, 1), (-1, -1)]


def pieces(dx, dy, sizes):
    lx, ly = sizes

    def beyond(d, length, near, far):
        return (-far if d > 0 else length - 1 + near, far - near + 1)

    def x(near, far=None):
        return beyond(dx, lx, near, far or near)

    def y(near, far=None):
        return beyond(dy, ly, near, far or near)

    def one(cx, cy):
        return VEL.index((cx, cy, 0)), 1

    every = (0, 19)
    if dy == 0:
        cells = [
            (1, every, x(1), (0, ly)),
            (1, every, x(2, 3), (0, 1)),
            (1, every, x(2, 3), (ly - 1, 1)),
            (1, one(dx, -1), x(4), (0, 1)),
            (1, one(dx, 1), x(4), (ly - 1, 1)),
            (2, every, x(2), (1, ly - 2)),
            (2, one(dx, -1), x(3), (1, 1)),
            (2, one(dx, 1), x(3), (ly - 2, 1)),
        ]
    elif dx == 0:
        cells = [
            (1, every, (0, lx), y(1)),
            (1, every, (0, 1), y(2, 3)),
            (1, every, (lx - 1, 1), y(2, 3)),
            (1, one(-1, dy), (0, 1), y(4)),
            (1, one(1, dy), (lx - 1, 1), y(4)),
            (2, every, (1, lx - 2), y(2)),
            (2, one(-1, dy), (1, 1), y(3)),
            (2, one(1, dy), (lx - 2, 1), y(3)),
        ]
    else:
        cells = [
            (1, every, x(1), y(1, 3)),
            (1, every, x(2, 3), y(1)),
            (1, one(dx, dy), x(4), y(1)),
            (1, one(dx, dy), x(1), y(4)),
            (2, every, x(2), y(2)),
            (2, one(dx, dy), x(3), y(2)),
            (2, one(dx, dy), x(2), y(3)),
        ]
    return [(level, lo, n, layers, rows) for level, (lo, n), layers, rows in cells]


def place(a, b, sizes):
    lx, ly = sizes
    bx = (a >= lx) - (a < 0)
    by = (b >= ly) - (b < 0)
    a, b = a - bx * lx, b - by * ly
    return (bx, by), min(a + 1, lx - a, b + 1, ly - b, 2)


def linked(time, sizes):
    def rule(x, y):
        if time > 2:
            return True
        block, level = place(*x, sizes)
        other, beneath = place(*y, sizes)
        return block != other or block == (0, 0) or level < time or beneath < time

    return rule


def linked_inside(time, sizes):
    def rule(x, y):
        block, level = place(*y, sizes)
        return block == (0, 0) and level >= time

    return rule


def collide(f):
    pairs = [(q, OPP[q]) for q in range(1, 19) if q < OPP[q]]
    rho = f[0]
    moment = [None, None, None]
    for i, j in pairs:
        rho = rho + (f[i] + f[j])
        diff = f[i] - f[j]
        for axis in range(3):
            c = VEL[i][axis]
            if c:
                term = moment[axis]
                if term is None:
                    moment[axis] = diff if c > 0 else -diff
                else:
                    moment[axis] = term + diff if c > 0 else term - diff
    inverse = 1.0 / rho
    u = [m * inverse for m in moment]
    base = 1.0 - 1.5 * (u[0] * u[0] + u[1] * u[1] + u[2] * u[2])
    scaled = {w: (RELAX * w) * rho for w in set(WEIGHT)}
    keep = 1.0 - RELAX
    post = [None] * 19
    post[0] = keep * f[0] + scaled[WEIGHT[0]] * base
    for i, j in pairs:
        proj = None
        for axis in range(3):
            c = VEL[i][axis]
            if c:
                if proj is None:
                    proj = u[axis] if c > 0 else -u[axis]
                else:
                    proj = proj + u[axis] if c > 0 else proj - u[axis]
        even = scaled[WEIGHT[i]] * (base + 4.5 * (proj * proj))
        odd = scaled[WEIGHT[i]] * (3.0 * proj)
        post[i] = keep * f[i] + (even + odd)
        post[j] = keep * f[j] + (even - odd)
    return post


def stream(buf, corner, a, row, rule):
    layer, base = corner[0] + a, corner[1] + row
    shape = (8, buf.shape[-1])
    rows = lax.broadcasted_iota(jnp.int32, shape, 0)
    masks = {}

    def open_rows(pattern):
        if pattern not in masks:
            mask = None
            start = 0
            while start < 8:
                if pattern[start]:
                    end = start
                    while end < 8 and pattern[end]:
                        end += 1
                    part = None
                    if start > 0:
                        part = rows >= start
                    if end < 8:
                        part = rows < end if part is None else part & (rows < end)
                    mask = part if mask is None else mask | part
                    start = end
                else:
                    start += 1
            masks[pattern] = mask
        return masks[pattern]

    result = []
    for q, (cx, cy, cz) in enumerate(VEL):
        kept = buf[OPP[q], layer, base : base + 8, :]
        pattern = tuple(rule((a, row + r), (a - cx, row + r - cy)) for r in range(8))
        if q == 0 or not any(pattern):
            result.append(kept)
            continue
        source = buf[q, layer - cx, base - cy : base - cy + 8, :]
        if cz:
            source = pltpu.roll(source, cz % source.shape[-1], 1)
        carry = source == source
        if not all(pattern):
            carry = carry & open_rows(pattern)
        result.append(jnp.where(carry, source, kept))
    return result


def kernel(axes, sizes, pops_hbm, fluid_hbm, out, first, wet, own1, own2, s1, s2, p1, p2, p3, p4, *sems):
    in_sem, send_sem, recv_sem = sems
    lx, ly = sizes
    nx, ny = axes
    ix, iy = lax.axis_index("gx"), lax.axis_index("gy")
    has = {0: None, 1: iy < ny - 1, -1: iy > 0}
    lanes = first.shape[-1]
    solid = jnp.full((ly, lanes), jnp.nan, jnp.float32)

    def when(condition, action):
        if condition is None:
            action()
        else:
            pl.when(condition)(action)

    def target(dx, dy):
        return {"gx": lax.rem(ix + nx + dx, nx), "gy": iy + dy}

    fluid_in = pltpu.make_async_copy(fluid_hbm, wet, in_sem.at[lx])
    loads = [
        pltpu.make_async_copy(pops_hbm.at[:, a], first.at[:, a], in_sem.at[a]) for a in range(lx)
    ]

    barrier = pltpu.get_barrier_semaphore()
    for dx, dy in DIRECTIONS:
        when(
            has[dy],
            lambda dx=dx, dy=dy: pl.semaphore_signal(
                barrier, inc=1, device_id=target(dx, dy), device_id_type=pl.DeviceIdType.MESH
            ),
        )

    fluid_in.start()
    for load in loads:
        load.start()

    for edge, row in ((iy == 0, PAD - 8), (iy == ny - 1, PAD + ly)):

        @pl.when(edge)
        def _():
            for q in range(19):
                for a in range(lx + 2 * HALO):
                    p1[q, a, row : row + 8, :] = jnp.full((8, lanes), jnp.nan, jnp.float32)

    def message(level, dx, dy):
        source, into = ((s1, p1), (s2, p2))[level - 1]
        base = sum(len(pieces(*d, sizes)) for d in DIRECTIONS[: DIRECTIONS.index((dx, dy))])
        copies = []
        for i, (at, lo, n, (a, an), (b, bn)) in enumerate(pieces(dx, dy, sizes)):
            if at == level:
                copies.append(
                    pltpu.make_async_remote_copy(
                        src_ref=source.at[pl.ds(lo, n), pl.ds(a + dx * lx, an), pl.ds(b + dy * ly, bn)],
                        dst_ref=into.at[pl.ds(lo, n), pl.ds(HALO + a, an), pl.ds(PAD + b, bn)],
                        send_sem=send_sem.at[base + i],
                        recv_sem=recv_sem.at[base + i],
                        device_id=target(dx, dy),
                        device_id_type=pl.DeviceIdType.MESH,
                    )
                )
        return copies

    def each(condition, copies, action):
        when(condition, lambda: [getattr(c, action)() for c in copies] and None)

    fluid_in.wait()
    for a in sorted(range(lx), key=lambda a: min(a, lx - 1 - a)):
        loads[a].wait()
        f = [first[TO_REF[q], a] for q in range(19)]
        f[0] = jnp.where(wet[a] != 0, f[0], solid)
        for q, value in enumerate(collide(f)):
            own1[q, a, PAD : PAD + ly, :] = value
            p1[q, HALO + a, PAD : PAD + ly, :] = value

    def part(source, into, a, time):
        f = stream(source, (0, PAD), a, 0, linked_inside(time, sizes))
        for q, value in enumerate(f):
            into[OPP[q], a] = jnp.where(wet[a] != 0, value, solid)
        return f

    for a in range(lx):
        f = part(own1, s1, a, 1)
        if 0 < a < lx - 1:
            for q, value in enumerate(collide(f)):
                own2[q, a, PAD : PAD + ly, :] = value

    peers = 2 + 3 * (iy > 0).astype(jnp.int32) + 3 * (iy < ny - 1).astype(jnp.int32)
    pl.semaphore_wait(barrier, peers)
    for d in DIRECTIONS:
        each(has[d[1]], message(1, *d), "start")
    for a in range(1, lx - 1):
        part(own2, s2, a, 2)
    for d in DIRECTIONS:
        each(has[d[1]], message(2, *d), "start")

    def advance(source, into, time, a, row, lo=0, hi=8):
        f = stream(source, (HALO, PAD), a, row, linked(time, sizes))
        for q, value in enumerate(collide(f)):
            into[q, HALO + a, PAD + row + lo : PAD + row + hi, :] = value[lo:hi]

    def rows(ring):
        return sorted({-ring, ly + ring - 8})

    for d in DIRECTIONS:
        each(has[-d[1]], message(1, *d), "wait_recv")
    for a in range(lx):
        for row in rows(3 if a in (0, lx - 1) else 1):
            advance(p1, p2, 1, a, row)
    for a in (-1, lx):
        for row in rows(3):
            advance(p1, p2, 1, a, row)
    for a in (-3, -2, lx + 1, lx + 2):
        advance(p1, p2, 1, a, -1, 0, 2)
        advance(p1, p2, 1, a, ly - 7, 6, 8)
    for d in DIRECTIONS:
        each(has[-d[1]], message(2, *d), "wait_recv")
    for a in range(-2, lx + 2):
        for row in rows(2):
            advance(p2, p3, 2, a, row)
    for a in range(-1, lx + 1):
        for row in rows(1):
            advance(p3, p4, 3, a, row)
    for a in range(lx):
        f = stream(p4, (HALO, PAD), a, 0, linked(4, sizes))
        for q in range(19):
            out[TO_REF[q], a] = jnp.where(wet[a] != 0, f[q], first[TO_REF[q], a])
    for level in (1, 2):
        for d in DIRECTIONS:
            each(has[d[1]], message(level, *d), "wait_send")


def write_out(source, target, sem):
    copies = [
        pltpu.make_async_copy(source.at[:, a], target.at[:, a], sem.at[a])
        for a in range(source.shape[1])
    ]
    for copy in copies:
        copy.start()
    for copy in copies:
        copy.wait()


def per_device(axes, populations, fluid):
    sizes = fluid.shape[:2]
    lx, ly = sizes
    nz = fluid.shape[2]
    count = sum(len(pieces(dx, dy, sizes)) for dx, dy in DIRECTIONS)
    dma = pltpu.SemaphoreType.DMA
    block = pltpu.VMEM(populations.shape, jnp.float32)
    tall = pltpu.VMEM((19, lx, ly + 2 * PAD, nz), jnp.float32)
    wide = pltpu.VMEM((19, lx + 2 * HALO, ly + 2 * PAD, nz), jnp.float32)
    result = pl.pallas_call(
        functools.partial(kernel, axes, sizes),
        out_shape=pltpu.VMEM(populations.shape, populations.dtype),
        in_specs=[pl.BlockSpec(memory_space=pl.ANY)] * 2,
        out_specs=pl.BlockSpec(memory_space=pltpu.VMEM),
        scratch_shapes=[block, pltpu.VMEM(fluid.shape, jnp.int32), tall, tall, block, block]
        + [wide] * STEPS
        + [dma((lx + 1,)), dma((count,)), dma((count,))],
        compiler_params=pltpu.CompilerParams(
            collective_id=0, has_side_effects=True, vmem_limit_bytes=60 * 1024 * 1024
        ),
    )(populations, fluid)
    return pl.pallas_call(
        write_out,
        out_shape=jax.ShapeDtypeStruct(populations.shape, populations.dtype),
        in_specs=[pl.BlockSpec(memory_space=pltpu.VMEM)],
        out_specs=pl.BlockSpec(memory_space=pl.ANY),
        scratch_shapes=[dma((lx,))],
        compiler_params=pltpu.CompilerParams(vmem_limit_bytes=16 * 2**20),
    )(result)


def solution(mesh):
    axes = (mesh.shape["gx"], mesh.shape["gy"])
    return jax.shard_map(
        functools.partial(per_device, axes),
        mesh=mesh,
        in_specs=(P(None, "gx", "gy", None), P("gx", "gy", None)),
        out_specs=P(None, "gx", "gy", None),
        check_vma=False,
    )
```

time: 18.5 us -> 15.3 us (0.83)
  the two profiles are of different devices: /device:TPU:1 before, /device:TPU:0 now
where the time goes in v2:
time: 15.3 us; the launch traced here: 15.1 us
  Pallas kernels  15.1 us (99%)
    pallas_call x1, Pallas kernels, per_device(): pl.pallas_call(functools.partial(kernel, axes, sizes), out_shape=pltpu.VM...  14.3 us
    pallas_call x1, Pallas kernels, per_device(): pl.pallas_call(write_out, out_shape=jax.ShapeDtypeStruct(populations.shap...  0.75 us

profile of v2, /device:TPU:0, one launch (start us, length us, event | category | flops | bytes accessed | tf_op | source)
XLA Modules:
  0.0 15.1 jit_solution(10216918283417261804)
XLA Ops:
  0.0 14.3 %shard_map.28.source = f32[19,4,8,128]{3,2,1,0:T(8,128)S(1)} custom-call(f32[19,4,8,128]{3,2,1,0:T(8,128)} %pops_hbm.1, s32[4,8,128]{2,1,0:T(8,128)} %fluid_hbm.1), custom_call_target="tpu_custom_call" | custom-call | tf_op jit(solution)/shard_map/pallas_call | solution.py:345
  14.3 0.7 %shard_map.29 = f32[19,4,8,128]{3,2,1,0:T(8,128)} custom-call(f32[19,4,8,128]{3,2,1,0:T(8,128)S(1)} %shard_map.28.source), custom_call_target="tpu_custom_call" | custom-call | tf_op jit(solution)/shard_map/pallas_call | solution.py:357

commit v3 on v2

--- a/solution.py
+++ b/solution.py
@@ -192,7 +192,7 @@
 
 
 def kernel(axes, sizes, pops_hbm, fluid_hbm, out, first, wet, own1, own2, s1, s2, p1, p2, p3, p4, *sems):
-    in_sem, send_sem, recv_sem = sems
+    in_sem, send_sem, recv_sem, late_sem = sems
     lx, ly = sizes
     nx, ny = axes
     ix, iy = lax.axis_index("gx"), lax.axis_index("gy")
@@ -215,32 +215,45 @@
     ]
 
     barrier = pltpu.get_barrier_semaphore()
+    is_first, is_last = ix == 0, ix == nx - 1
+    columns = 1 + (iy > 0).astype(jnp.int32) + (iy < ny - 1).astype(jnp.int32)
+
+    def greet(sem, dx, dy):
+        pl.semaphore_signal(
+            sem, inc=1, device_id=target(dx, dy), device_id_type=pl.DeviceIdType.MESH
+        )
+
     for dx, dy in DIRECTIONS:
-        when(
-            has[dy],
-            lambda dx=dx, dy=dy: pl.semaphore_signal(
-                barrier, inc=1, device_id=target(dx, dy), device_id_type=pl.DeviceIdType.MESH
-            ),
-        )
-
-    fluid_in.start()
-    for load in loads:
-        load.start()
-
-    for edge, row in ((iy == 0, PAD - 8), (iy == ny - 1, PAD + ly)):
-
-        @pl.when(edge)
+        condition = has[dy]
+        if dx > 0:
+            condition = ix < nx - 2 if condition is None else jnp.logical_and(condition, ix < nx - 2)
+        when(condition, lambda dx=dx, dy=dy: greet(barrier, dx, dy))
+
+    def wait_barrier():
+        ends = jnp.logical_or(is_first, is_last)
+        pl.semaphore_wait(barrier, jnp.where(ends, 2, 3) * columns - 1)
+
+        @pl.when(ix >= nx - 2)
         def _():
-            for q in range(19):
-                for a in range(lx + 2 * HALO):
-                    p1[q, a, row : row + 8, :] = jnp.full((8, lanes), jnp.nan, jnp.float32)
-
-    def message(level, dx, dy):
+            for dy in (0, 1, -1):
+                when(has[dy], lambda dy=dy: greet(late_sem, 1, dy))
+
+    def fill_walls():
+        for edge, row in ((iy == 0, PAD - 8), (iy == ny - 1, PAD + ly)):
+
+            @pl.when(edge)
+            def _():
+                for q in range(19):
+                    for a in range(lx + 2 * HALO):
+                        p1[q, a, row : row + 8, :] = jnp.full((8, lanes), jnp.nan, jnp.float32)
+
+    def message(level, dx, dy, nearest=None):
         source, into = ((s1, p1), (s2, p2))[level - 1]
         base = sum(len(pieces(*d, sizes)) for d in DIRECTIONS[: DIRECTIONS.index((dx, dy))])
         copies = []
         for i, (at, lo, n, (a, an), (b, bn)) in enumerate(pieces(dx, dy, sizes)):
-            if at == level:
+            seam = an == 1 and a in (-1, lx)
+            if at == level and nearest in (None, seam):
                 copies.append(
                     pltpu.make_async_remote_copy(
                         src_ref=source.at[pl.ds(lo, n), pl.ds(a + dx * lx, an), pl.ds(b + dy * ly, bn)],
@@ -253,11 +266,10 @@
                 )
         return copies
 
-    def each(condition, copies, action):
-        when(condition, lambda: [getattr(c, action)() for c in copies] and None)
-
-    fluid_in.wait()
-    for a in sorted(range(lx), key=lambda a: min(a, lx - 1 - a)):
+    def each(dy, copies, action):
+        when(has[dy], lambda: [getattr(c, action)() for c in copies] and None)
+
+    def post_layer(a):
         loads[a].wait()
         f = [first[TO_REF[q], a] for q in range(19)]
         f[0] = jnp.where(wet[a] != 0, f[0], solid)
@@ -271,21 +283,12 @@
             into[OPP[q], a] = jnp.where(wet[a] != 0, value, solid)
         return f
 
-    for a in range(lx):
+    def part_layer(a):
         f = part(own1, s1, a, 1)
         if 0 < a < lx - 1:
             for q, value in enumerate(collide(f)):
                 own2[q, a, PAD : PAD + ly, :] = value
 
-    peers = 2 + 3 * (iy > 0).astype(jnp.int32) + 3 * (iy < ny - 1).astype(jnp.int32)
-    pl.semaphore_wait(barrier, peers)
-    for d in DIRECTIONS:
-        each(has[d[1]], message(1, *d), "start")
-    for a in range(1, lx - 1):
-        part(own2, s2, a, 2)
-    for d in DIRECTIONS:
-        each(has[d[1]], message(2, *d), "start")
-
     def advance(source, into, time, a, row, lo=0, hi=8):
         f = stream(source, (HALO, PAD), a, row, linked(time, sizes))
         for q, value in enumerate(collide(f)):
@@ -294,32 +297,115 @@
     def rows(ring):
         return sorted({-ring, ly + ring - 8})
 
-    for d in DIRECTIONS:
-        each(has[-d[1]], message(1, *d), "wait_recv")
-    for a in range(lx):
-        for row in rows(3 if a in (0, lx - 1) else 1):
-            advance(p1, p2, 1, a, row)
-    for a in (-1, lx):
-        for row in rows(3):
-            advance(p1, p2, 1, a, row)
-    for a in (-3, -2, lx + 1, lx + 2):
-        advance(p1, p2, 1, a, -1, 0, 2)
-        advance(p1, p2, 1, a, ly - 7, 6, 8)
-    for d in DIRECTIONS:
-        each(has[-d[1]], message(2, *d), "wait_recv")
-    for a in range(-2, lx + 2):
-        for row in rows(2):
-            advance(p2, p3, 2, a, row)
-    for a in range(-1, lx + 1):
-        for row in rows(1):
-            advance(p3, p4, 3, a, row)
+    def second(a):
+        if a in (-1, 0, lx - 1, lx):
+            for row in rows(3):
+                advance(p1, p2, 1, a, row)
+        elif 0 < a < lx - 1:
+            for row in rows(1):
+                advance(p1, p2, 1, a, row)
+        else:
+            advance(p1, p2, 1, a, -1, 0, 2)
+            advance(p1, p2, 1, a, ly - 7, 6, 8)
+
+    def variant(side):
+        ys = (0, 1, -1)
+        away, home = [(side, dy) for dy in ys], [(-side, dy) for dy in ys]
+        across = [(0, 1), (0, -1)]
+        order = [a if side < 0 else lx - 1 - a for a in range(lx)]
+
+        def layers(lo, hi):
+            return [a if side < 0 else lx - 1 - a for a in range(lo, hi + 1)]
+
+        fluid_in.start()
+        for a in order:
+            loads[a].start()
+        fill_walls()
+        fluid_in.wait()
+        post_layer(order[0])
+        post_layer(order[1])
+        part_layer(order[0])
+        wait_barrier()
+
+        def send(directions, level, nearest=None):
+            for d in directions:
+                each(d[1], message(level, *d, nearest), "start")
+
+        if side < 0:
+            pl.when(jnp.logical_not(is_first))(lambda: send(away, 1, True))
+        else:
+            send(away, 1, True)
+        for a in order[2:]:
+            post_layer(a)
+        for a in order[1:]:
+            part_layer(a)
+        if side < 0:
+            pl.when(jnp.logical_not(is_first))(lambda: send(away, 1, False))
+            send(across, 1)
+            send(home, 1)
+        else:
+            send(away, 1, False)
+            send(across, 1)
+            pl.when(jnp.logical_not(is_last))(lambda: send(home, 1))
+        for a in order[1:-1]:
+            part(own2, s2, a, 2)
+        if side < 0:
+            pl.when(jnp.logical_not(is_first))(lambda: send(away, 2))
+            send(across, 2)
+            send(home, 2)
+
+            @pl.when(is_first)
+            def _():
+                pl.semaphore_wait(late_sem, columns)
+                send(away, 1)
+                send(away, 2)
+        else:
+            send(away, 2)
+            send(across, 2)
+            pl.when(jnp.logical_not(is_last))(lambda: send(home, 2))
+
+            @pl.when(is_last)
+            def _():
+                pl.semaphore_wait(late_sem, columns)
+                send(home, 1)
+                send(home, 2)
+
+        def receive(directions, level):
+            for d in directions:
+                each(-d[1], message(level, *d), "wait_recv")
+
+        receive(across, 1)
+        receive(away, 1)
+        for a in layers(1, lx + 2):
+            second(a)
+        receive(across, 2)
+        receive(away, 2)
+        for a in layers(2, lx + 1):
+            for row in rows(2):
+                advance(p2, p3, 2, a, row)
+        for a in layers(3, lx):
+            for row in rows(1):
+                advance(p3, p4, 3, a, row)
+        receive(home, 1)
+        for a in layers(-3, 0):
+            second(a)
+        receive(home, 2)
+        for a in layers(-2, 1):
+            for row in rows(2):
+                advance(p2, p3, 2, a, row)
+        for a in layers(-1, 2):
+            for row in rows(1):
+                advance(p3, p4, 3, a, row)
+
+    pl.when(lax.rem(ix, 2) == 0)(lambda: variant(-1))
+    pl.when(lax.rem(ix, 2) == 1)(lambda: variant(1))
     for a in range(lx):
         f = stream(p4, (HALO, PAD), a, 0, linked(4, sizes))
         for q in range(19):
             out[TO_REF[q], a] = jnp.where(wet[a] != 0, f[q], first[TO_REF[q], a])
     for level in (1, 2):
         for d in DIRECTIONS:
-            each(has[d[1]], message(level, *d), "wait_send")
+            each(d[1], message(level, *d), "wait_send")
 
 
 def write_out(source, target, sem):
@@ -349,7 +435,7 @@
         out_specs=pl.BlockSpec(memory_space=pltpu.VMEM),
         scratch_shapes=[block, pltpu.VMEM(fluid.shape, jnp.int32), tall, tall, block, block]
         + [wide] * STEPS
-        + [dma((lx + 1,)), dma((count,)), dma((count,))],
+        + [dma((lx + 1,)), dma((count,)), dma((count,)), pltpu.SemaphoreType.REGULAR],
         compiler_params=pltpu.CompilerParams(
             collective_id=0, has_side_effects=True, vmem_limit_bytes=60 * 1024 * 1024
         ),

time: 15.3 us -> 14.2 us (0.928)
  Pallas kernels: 15.1 us -> 14 us
    pallas_call x1, Pallas kernels: 14.3 us -> 13.2 us  [per_device(): pl.pallas_call(functools.partial(kernel, axes, sizes), out_shape=pltpu.VM...]
where the time goes in v3:
time: 14.2 us; the launch traced here: 14 us
  Pallas kernels  14 us (99%)
    pallas_call x1, Pallas kernels, per_device(): pl.pallas_call(functools.partial(kernel, axes, sizes), out_shape=pltpu.VM...  13.2 us
    pallas_call x1, Pallas kernels, per_device(): pl.pallas_call(write_out, out_shape=jax.ShapeDtypeStruct(populations.shap...  0.75 us

profile of v3, /device:TPU:0, one launch (start us, length us, event | category | flops | bytes accessed | tf_op | source)
XLA Modules:
  0.0 14.0 jit_solution(8456763755940875988)
XLA Ops:
  0.0 13.2 %shard_map.28.source = f32[19,4,8,128]{3,2,1,0:T(8,128)S(1)} custom-call(f32[19,4,8,128]{3,2,1,0:T(8,128)} %pops_hbm.1, s32[4,8,128]{2,1,0:T(8,128)} %fluid_hbm.1), custom_call_target="tpu_custom_call" | custom-call | tf_op jit(solution)/shard_map/pallas_call | solution.py:431
  13.2 0.7 %shard_map.29 = f32[19,4,8,128]{3,2,1,0:T(8,128)} custom-call(f32[19,4,8,128]{3,2,1,0:T(8,128)S(1)} %shard_map.28.source), custom_call_target="tpu_custom_call" | custom-call | tf_op jit(solution)/shard_map/pallas_call | solution.py:443

commit v4 on v3

--- a/solution.py
+++ b/solution.py
@@ -192,7 +192,7 @@
 
 
 def kernel(axes, sizes, pops_hbm, fluid_hbm, out, first, wet, own1, own2, s1, s2, p1, p2, p3, p4, *sems):
-    in_sem, send_sem, recv_sem, late_sem = sems
+    tally, in_sem, send_sem, recv_sem, late_sem = sems
     lx, ly = sizes
     nx, ny = axes
     ix, iy = lax.axis_index("gx"), lax.axis_index("gy")
@@ -247,27 +247,34 @@
                     for a in range(lx + 2 * HALO):
                         p1[q, a, row : row + 8, :] = jnp.full((8, lanes), jnp.nan, jnp.float32)
 
-    def message(level, dx, dy, nearest=None):
+    def message(side, level, dx, dy, nearest=None):
         source, into = ((s1, p1), (s2, p2))[level - 1]
-        base = sum(len(pieces(*d, sizes)) for d in DIRECTIONS[: DIRECTIONS.index((dx, dy))])
         copies = []
-        for i, (at, lo, n, (a, an), (b, bn)) in enumerate(pieces(dx, dy, sizes)):
+        for at, lo, n, (a, an), (b, bn) in pieces(dx, dy, sizes):
             seam = an == 1 and a in (-1, lx)
             if at == level and nearest in (None, seam):
                 copies.append(
                     pltpu.make_async_remote_copy(
                         src_ref=source.at[pl.ds(lo, n), pl.ds(a + dx * lx, an), pl.ds(b + dy * ly, bn)],
                         dst_ref=into.at[pl.ds(lo, n), pl.ds(HALO + a, an), pl.ds(PAD + b, bn)],
-                        send_sem=send_sem.at[base + i],
-                        recv_sem=recv_sem.at[base + i],
+                        send_sem=send_sem.at[dy + 1],
+                        recv_sem=recv_sem.at[int(dx == side), level - 1, dy + 1],
                         device_id=target(dx, dy),
                         device_id_type=pl.DeviceIdType.MESH,
                     )
                 )
         return copies
 
-    def each(dy, copies, action):
-        when(has[dy], lambda: [getattr(c, action)() for c in copies] and None)
+    def amount(directions, levels):
+        return sum(
+            n * an * bn
+            for d in directions
+            for at, lo, n, (a, an), (b, bn) in pieces(*d, sizes)
+            if at in levels
+        )
+
+    def await_rows(sem, count):
+        pltpu.make_async_copy(tally.at[pl.ds(0, count)], tally.at[pl.ds(0, count)], sem).wait()
 
     def post_layer(a):
         loads[a].wait()
@@ -329,7 +336,8 @@
 
         def send(directions, level, nearest=None):
             for d in directions:
-                each(d[1], message(level, *d, nearest), "start")
+                copies = message(side, level, *d, nearest)
+                when(has[d[1]], lambda copies=copies: [c.start() for c in copies] and None)
 
         if side < 0:
             pl.when(jnp.logical_not(is_first))(lambda: send(away, 1, True))
@@ -370,26 +378,31 @@
                 send(home, 1)
                 send(home, 2)
 
-        def receive(directions, level):
-            for d in directions:
-                each(-d[1], message(level, *d), "wait_recv")
-
-        receive(across, 1)
-        receive(away, 1)
+        def receive(late, level):
+            dx = -side if late else side
+            for dy in (0, 1, -1):
+                directions = [(dx, dy)] if late or dy == 0 else [(dx, dy), (0, dy)]
+                when(
+                    has[-dy],
+                    lambda dy=dy, count=amount(directions, (level,)): await_rows(
+                        recv_sem.at[int(late), level - 1, dy + 1], count
+                    ),
+                )
+
+        receive(False, 1)
         for a in layers(1, lx + 2):
             second(a)
-        receive(across, 2)
-        receive(away, 2)
+        receive(False, 2)
         for a in layers(2, lx + 1):
             for row in rows(2):
                 advance(p2, p3, 2, a, row)
         for a in layers(3, lx):
             for row in rows(1):
                 advance(p3, p4, 3, a, row)
-        receive(home, 1)
+        receive(True, 1)
         for a in layers(-3, 0):
             second(a)
-        receive(home, 2)
+        receive(True, 2)
         for a in layers(-2, 1):
             for row in rows(2):
                 advance(p2, p3, 2, a, row)
@@ -403,9 +416,9 @@
         f = stream(p4, (HALO, PAD), a, 0, linked(4, sizes))
         for q in range(19):
             out[TO_REF[q], a] = jnp.where(wet[a] != 0, f[q], first[TO_REF[q], a])
-    for level in (1, 2):
-        for d in DIRECTIONS:
-            each(d[1], message(level, *d), "wait_send")
+    for dy in (0, 1, -1):
+        count = amount([d for d in DIRECTIONS if d[1] == dy], (1, 2))
+        when(has[dy], lambda dy=dy, count=count: await_rows(send_sem.at[dy + 1], count))
 
 
 def write_out(source, target, sem):
@@ -423,7 +436,7 @@
     sizes = fluid.shape[:2]
     lx, ly = sizes
     nz = fluid.shape[2]
-    count = sum(len(pieces(dx, dy, sizes)) for dx, dy in DIRECTIONS)
+    count = sum(n * a[1] * b[1] for d in DIRECTIONS for _, _, n, a, b in pieces(*d, sizes))
     dma = pltpu.SemaphoreType.DMA
     block = pltpu.VMEM(populations.shape, jnp.float32)
     tall = pltpu.VMEM((19, lx, ly + 2 * PAD, nz), jnp.float32)
@@ -435,7 +448,8 @@
         out_specs=pl.BlockSpec(memory_space=pltpu.VMEM),
         scratch_shapes=[block, pltpu.VMEM(fluid.shape, jnp.int32), tall, tall, block, block]
         + [wide] * STEPS
-        + [dma((lx + 1,)), dma((count,)), dma((count,)), pltpu.SemaphoreType.REGULAR],
+        + [pltpu.VMEM((count, nz), jnp.float32)]
+        + [dma((lx + 1,)), dma((3,)), dma((2, 2, 3)), pltpu.SemaphoreType.REGULAR],
         compiler_params=pltpu.CompilerParams(
             collective_id=0, has_side_effects=True, vmem_limit_bytes=60 * 1024 * 1024
         ),

time: 14.2 us -> 13.2 us (0.930)
  Pallas kernels: 14 us -> 13 us
    pallas_call x1, Pallas kernels: 13.2 us -> 12.2 us  [per_device(): pl.pallas_call(functools.partial(kernel, axes, sizes), out_shape=pltpu.VM...]
where the time goes in v4:
time: 13.2 us; the launch traced here: 13 us
  Pallas kernels  13 us (98%)
    pallas_call x1, Pallas kernels, per_device(): pl.pallas_call(functools.partial(kernel, axes, sizes), out_shape=pltpu.VM...  12.2 us
    pallas_call x1, Pallas kernels, per_device(): pl.pallas_call(write_out, out_shape=jax.ShapeDtypeStruct(populations.shap...  0.75 us

profile of v4, /device:TPU:0, one launch (start us, length us, event | category | flops | bytes accessed | tf_op | source)
XLA Modules:
  0.0 13.0 jit_solution(4754615050667838712)
XLA Ops:
  0.0 12.2 %shard_map.28.source = f32[19,4,8,128]{3,2,1,0:T(8,128)S(1)} custom-call(f32[19,4,8,128]{3,2,1,0:T(8,128)} %pops_hbm.1, s32[4,8,128]{2,1,0:T(8,128)} %fluid_hbm.1), custom_call_target="tpu_custom_call" | custom-call | tf_op jit(solution)/shard_map/pallas_call | solution.py:444
  12.2 0.7 %shard_map.29 = f32[19,4,8,128]{3,2,1,0:T(8,128)} custom-call(f32[19,4,8,128]{3,2,1,0:T(8,128)S(1)} %shard_map.28.source), custom_call_target="tpu_custom_call" | custom-call | tf_op jit(solution)/shard_map/pallas_call | solution.py:457

commit v5 on v4

--- a/solution.py
+++ b/solution.py
@@ -257,13 +257,28 @@
                     pltpu.make_async_remote_copy(
                         src_ref=source.at[pl.ds(lo, n), pl.ds(a + dx * lx, an), pl.ds(b + dy * ly, bn)],
                         dst_ref=into.at[pl.ds(lo, n), pl.ds(HALO + a, an), pl.ds(PAD + b, bn)],
-                        send_sem=send_sem.at[dy + 1],
-                        recv_sem=recv_sem.at[int(dx == side), level - 1, dy + 1],
+                        send_sem=send_sem,
+                        recv_sem=recv_sem.at[(int(dx == side) if dx else 2), level - 1],
                         device_id=target(dx, dy),
                         device_id_type=pl.DeviceIdType.MESH,
                     )
                 )
         return copies
+
+    def forward(side, level, dy):
+        buf = (p1, p2)[level - 1]
+        return [
+            pltpu.make_async_remote_copy(
+                src_ref=buf.at[pl.ds(lo, n), pl.ds(HALO + a - side * lx, an), pl.ds(PAD + b, bn)],
+                dst_ref=buf.at[pl.ds(lo, n), pl.ds(HALO + a, an), pl.ds(PAD + b, bn)],
+                send_sem=send_sem,
+                recv_sem=recv_sem.at[0, level - 1],
+                device_id=target(-side, 0),
+                device_id_type=pl.DeviceIdType.MESH,
+            )
+            for at, lo, n, (a, an), (b, bn) in pieces(-side, dy, sizes)
+            if at == level
+        ]
 
     def amount(directions, levels):
         return sum(
@@ -275,6 +290,12 @@
 
     def await_rows(sem, count):
         pltpu.make_async_copy(tally.at[pl.ds(0, count)], tally.at[pl.ds(0, count)], sem).wait()
+
+    def await_by_sides(sem, base, extra):
+        for sides in range(3):
+            if base + sides * extra:
+                count = base + sides * extra
+                pl.when(columns == 1 + sides)(lambda count=count: await_rows(sem, count))
 
     def post_layer(a):
         loads[a].wait()
@@ -315,9 +336,25 @@
             advance(p1, p2, 1, a, -1, 0, 2)
             advance(p1, p2, 1, a, ly - 7, 6, 8)
 
+    def third(layers):
+        for a in layers:
+            for row in rows(2):
+                advance(p2, p3, 2, a, row)
+
+    def fourth(layers):
+        for a in layers:
+            for row in rows(1):
+                advance(p3, p4, 3, a, row)
+
+    def last(layers):
+        for a in layers:
+            f = stream(p4, (HALO, PAD), a, 0, linked(4, sizes))
+            for q in range(19):
+                out[TO_REF[q], a] = jnp.where(wet[a] != 0, f[q], first[TO_REF[q], a])
+
     def variant(side):
-        ys = (0, 1, -1)
-        away, home = [(side, dy) for dy in ys], [(-side, dy) for dy in ys]
+        ys = (-1, 0, 1)
+        away, home = [(side, dy) for dy in ys], [(-side, 0)]
         across = [(0, 1), (0, -1)]
         order = [a if side < 0 else lx - 1 - a for a in range(lx)]
 
@@ -349,87 +386,78 @@
             part_layer(a)
         if side < 0:
             pl.when(jnp.logical_not(is_first))(lambda: send(away, 1, False))
-            send(across, 1)
-            send(home, 1)
         else:
             send(away, 1, False)
-            send(across, 1)
-            pl.when(jnp.logical_not(is_last))(lambda: send(home, 1))
         for a in order[1:-1]:
             part(own2, s2, a, 2)
         if side < 0:
             pl.when(jnp.logical_not(is_first))(lambda: send(away, 2))
-            send(across, 2)
-            send(home, 2)
+            for level in (1, 2):
+                send(across + home, level)
+
+        else:
+            send(away, 2)
+            for level in (1, 2):
+                send(across, level)
+                pl.when(jnp.logical_not(is_last))(lambda level=level: send(home, level))
+
+            @pl.when(is_last)
+            def _():
+                pl.semaphore_wait(late_sem, columns)
+                send(home, 1)
+                send(home, 2)
+
+        def receive(late, level):
+            dx = -side if late else side
+            await_by_sides(
+                recv_sem.at[int(late), level - 1],
+                amount([(dx, 0)], (level,)),
+                amount([(dx, 1)], (level,)),
+            )
+
+        if side < 0:
 
             @pl.when(is_first)
             def _():
                 pl.semaphore_wait(late_sem, columns)
                 send(away, 1)
                 send(away, 2)
-        else:
-            send(away, 2)
-            send(across, 2)
-            pl.when(jnp.logical_not(is_last))(lambda: send(home, 2))
-
-            @pl.when(is_last)
-            def _():
-                pl.semaphore_wait(late_sem, columns)
-                send(home, 1)
-                send(home, 2)
-
-        def receive(late, level):
-            dx = -side if late else side
-            for dy in (0, 1, -1):
-                directions = [(dx, dy)] if late or dy == 0 else [(dx, dy), (0, dy)]
-                when(
-                    has[-dy],
-                    lambda dy=dy, count=amount(directions, (level,)): await_rows(
-                        recv_sem.at[int(late), level - 1, dy + 1], count
-                    ),
-                )
-
+
+        for level in (1, 2):
+            await_by_sides(recv_sem.at[2, level - 1], 0, amount([(0, 1)], (level,)))
+            for dy in (1, -1):
+                copies = forward(side, level, dy)
+                when(has[-dy], lambda copies=copies: [c.start() for c in copies] and None)
         receive(False, 1)
         for a in layers(1, lx + 2):
             second(a)
         receive(False, 2)
-        for a in layers(2, lx + 1):
-            for row in rows(2):
-                advance(p2, p3, 2, a, row)
-        for a in layers(3, lx):
-            for row in rows(1):
-                advance(p3, p4, 3, a, row)
+        third(layers(2, lx + 1))
+        fourth(layers(3, lx))
         receive(True, 1)
         for a in layers(-3, 0):
             second(a)
+        third(layers(0, 1))
+        fourth(layers(1, 2))
+        last(layers(2, lx - 1))
         receive(True, 2)
-        for a in layers(-2, 1):
-            for row in rows(2):
-                advance(p2, p3, 2, a, row)
-        for a in layers(-1, 2):
-            for row in rows(1):
-                advance(p3, p4, 3, a, row)
+        third(layers(-2, -1))
+        fourth(layers(-1, 0))
+        last(layers(0, 1))
 
     pl.when(lax.rem(ix, 2) == 0)(lambda: variant(-1))
     pl.when(lax.rem(ix, 2) == 1)(lambda: variant(1))
-    for a in range(lx):
-        f = stream(p4, (HALO, PAD), a, 0, linked(4, sizes))
-        for q in range(19):
-            out[TO_REF[q], a] = jnp.where(wet[a] != 0, f[q], first[TO_REF[q], a])
-    for dy in (0, 1, -1):
-        count = amount([d for d in DIRECTIONS if d[1] == dy], (1, 2))
-        when(has[dy], lambda dy=dy, count=count: await_rows(send_sem.at[dy + 1], count))
+    await_by_sides(
+        send_sem,
+        amount([d for d in DIRECTIONS if d[1] == 0], (1, 2)),
+        amount([d for d in DIRECTIONS if d[1] == 1], (1, 2)),
+    )
 
 
 def write_out(source, target, sem):
-    copies = [
-        pltpu.make_async_copy(source.at[:, a], target.at[:, a], sem.at[a])
-        for a in range(source.shape[1])
-    ]
-    for copy in copies:
-        copy.start()
-    for copy in copies:
-        copy.wait()
+    copy = pltpu.make_async_copy(source, target, sem)
+    copy.start()
+    copy.wait()
 
 
 def per_device(axes, populations, fluid):
@@ -449,7 +477,7 @@
         scratch_shapes=[block, pltpu.VMEM(fluid.shape, jnp.int32), tall, tall, block, block]
         + [wide] * STEPS
         + [pltpu.VMEM((count, nz), jnp.float32)]
-        + [dma((lx + 1,)), dma((3,)), dma((2, 2, 3)), pltpu.SemaphoreType.REGULAR],
+        + [dma((lx + 1,)), dma, dma((3, 2)), pltpu.SemaphoreType.REGULAR],
         compiler_params=pltpu.CompilerParams(
             collective_id=0, has_side_effects=True, vmem_limit_bytes=60 * 1024 * 1024
         ),
@@ -459,7 +487,7 @@
         out_shape=jax.ShapeDtypeStruct(populations.shape, populations.dtype),
         in_specs=[pl.BlockSpec(memory_space=pltpu.VMEM)],
         out_specs=pl.BlockSpec(memory_space=pl.ANY),
-        scratch_shapes=[dma((lx,))],
+        scratch_shapes=[dma],
         compiler_params=pltpu.CompilerParams(vmem_limit_bytes=16 * 2**20),
     )(result)
 

time: 13.2 us -> 12.6 us (0.955)
  Pallas kernels: 13 us -> 12.3 us
    pallas_call x1, Pallas kernels: 12.2 us -> 11.6 us  [per_device(): pl.pallas_call(functools.partial(kernel, axes, sizes), out_shape=pltpu.VM...]
where the time goes in v5:
time: 12.6 us; the launch traced here: 12.3 us
  Pallas kernels  12.3 us (98%)
    pallas_call x1, Pallas kernels, per_device(): pl.pallas_call(functools.partial(kernel, axes, sizes), out_shape=pltpu.VM...  11.6 us
    pallas_call x1, Pallas kernels, per_device(): pl.pallas_call(write_out, out_shape=jax.ShapeDtypeStruct(populations.shap...  0.73 us

profile of v5, /device:TPU:0, one launch (start us, length us, event | category | flops | bytes accessed | tf_op | source)
XLA Modules:
  0.0 12.3 jit_solution(7406099986810697737)
XLA Ops:
  0.0 11.6 %shard_map.28.source = f32[19,4,8,128]{3,2,1,0:T(8,128)S(1)} custom-call(f32[19,4,8,128]{3,2,1,0:T(8,128)} %pops_hbm.1, s32[4,8,128]{2,1,0:T(8,128)} %fluid_hbm.1), custom_call_target="tpu_custom_call" | custom-call | tf_op jit(solution)/shard_map/pallas_call | solution.py:472
  11.6 0.7 %shard_map.29 = f32[19,4,8,128]{3,2,1,0:T(8,128)} custom-call(f32[19,4,8,128]{3,2,1,0:T(8,128)S(1)} %shard_map.28.source), custom_call_target="tpu_custom_call" | custom-call | tf_op jit(solution)/shard_map/pallas_call | solution.py:485

commit v6 on v5

--- a/solution.py
+++ b/solution.py
@@ -127,10 +127,11 @@
     inverse = 1.0 / rho
     u = [m * inverse for m in moment]
     base = 1.0 - 1.5 * (u[0] * u[0] + u[1] * u[1] + u[2] * u[2])
-    scaled = {w: (RELAX * w) * rho for w in set(WEIGHT)}
+    level = {w: ((RELAX * w) * rho) * base for w in sorted(set(WEIGHT))}
+    slope = {w: (3.0 * RELAX * w) * rho for w in sorted(set(WEIGHT[1:]))}
     keep = 1.0 - RELAX
     post = [None] * 19
-    post[0] = keep * f[0] + scaled[WEIGHT[0]] * base
+    post[0] = keep * f[0] + level[WEIGHT[0]]
     for i, j in pairs:
         proj = None
         for axis in range(3):
@@ -140,8 +141,8 @@
                     proj = u[axis] if c > 0 else -u[axis]
                 else:
                     proj = proj + u[axis] if c > 0 else proj - u[axis]
-        even = scaled[WEIGHT[i]] * (base + 4.5 * (proj * proj))
-        odd = scaled[WEIGHT[i]] * (3.0 * proj)
+        odd = slope[WEIGHT[i]] * proj
+        even = level[WEIGHT[i]] + (1.5 * proj) * odd
         post[i] = keep * f[i] + (even + odd)
         post[j] = keep * f[j] + (even - odd)
     return post
@@ -376,27 +377,33 @@
                 copies = message(side, level, *d, nearest)
                 when(has[d[1]], lambda copies=copies: [c.start() for c in copies] and None)
 
-        if side < 0:
-            pl.when(jnp.logical_not(is_first))(lambda: send(away, 1, True))
-        else:
-            send(away, 1, True)
+        free = jnp.logical_not(is_first) if side < 0 else ix >= 0
+        down, face, up = [(side, -1)], [(side, 0)], [(side, 1)]
+
+        def leading(level, nearest=None):
+            pl.when(free)(lambda: send(down, level, nearest))
+
+        def facing(level, nearest=None):
+            pl.when(jnp.logical_and(free, iy == 0))(lambda: send(face, level, nearest))
+
+        leading(1, True)
+        facing(1, True)
         for a in order[2:]:
             post_layer(a)
         for a in order[1:]:
             part_layer(a)
-        if side < 0:
-            pl.when(jnp.logical_not(is_first))(lambda: send(away, 1, False))
-        else:
-            send(away, 1, False)
+        leading(1, False)
+        facing(1, False)
         for a in order[1:-1]:
             part(own2, s2, a, 2)
+        leading(2)
+        pl.when(jnp.logical_and(free, iy > 0))(lambda: send(face, 1))
+        pl.when(free)(lambda: (send(face, 2), send(up, 1), send(up, 2), None)[3])
         if side < 0:
-            pl.when(jnp.logical_not(is_first))(lambda: send(away, 2))
             for level in (1, 2):
                 send(across + home, level)
 
         else:
-            send(away, 2)
             for level in (1, 2):
                 send(across, level)
                 pl.when(jnp.logical_not(is_last))(lambda level=level: send(home, level))

time: 12.6 us -> 12.5 us (level)
  no operation moved by 1% of the time
where the time goes in v6:
time: 12.5 us; the launch traced here: 12.2 us
  Pallas kernels  12.2 us (98%)
    pallas_call x1, Pallas kernels, per_device(): pl.pallas_call(functools.partial(kernel, axes, sizes), out_shape=pltpu.VM...  11.5 us
    pallas_call x1, Pallas kernels, per_device(): pl.pallas_call(write_out, out_shape=jax.ShapeDtypeStruct(populations.shap...  0.73 us

profile of v6, /device:TPU:0, one launch (start us, length us, event | category | flops | bytes accessed | tf_op | source)
XLA Modules:
  0.0 12.2 jit_solution(2765907263369838262)
XLA Ops:
  0.0 11.5 %shard_map.28.source = f32[19,4,8,128]{3,2,1,0:T(8,128)S(1)} custom-call(f32[19,4,8,128]{3,2,1,0:T(8,128)} %pops_hbm.1, s32[4,8,128]{2,1,0:T(8,128)} %fluid_hbm.1), custom_call_target="tpu_custom_call" | custom-call | tf_op jit(solution)/shard_map/pallas_call | solution.py:479
  11.5 0.7 %shard_map.29 = f32[19,4,8,128]{3,2,1,0:T(8,128)} custom-call(f32[19,4,8,128]{3,2,1,0:T(8,128)S(1)} %shard_map.28.source), custom_call_target="tpu_custom_call" | custom-call | tf_op jit(solution)/shard_map/pallas_call | solution.py:492
